TPU v7x, 32 devices: a whole 2x2x4 slice. The times are simulated.
32 devices in a mesh: leaf: 8 (over z, y), rhs: 4 (over x, core).
Axes of the slice: x: 2, y: 2, z: 4, core: 2. Of those that a mesh axis runs over, the one named last changes fastest.
Arguments:
- right_sides: float32 [64, 8192], P('rhs', 'leaf'), may hold values from -8 to 8
- leaf_inverse: float32 [8192, 1024], P('leaf', 'rhs'), may hold values from -1 to 5, as said below
- bases: bfloat16 [3, 128, 8192], P(None, None, 'leaf'), may hold values from -1 to 1
- ordering: int32 [8, 1024], P('leaf'), may hold values from 0 to 1023, as said below
Outputs:
- solution: float32 [64, 8192], P('rhs', 'leaf')
Inputs may be any that keep to these rules, and one draw needn't show every extreme that they name: `leaf_inverse`: each leaf's block of 1024 rows is symmetric positive definite. `ordering`: each row is a permutation of 0 to 1023.
All inputs are finite; a program needn't handle non-finite values.
Results may differ from a plain program's by a relative error of at most 0.0003.
Values sent between devices are 32-bit elements; how exact they have to be, the bound alone decides.
A program may use at most 64 MiB of HBM per device.

v0:
```python
import jax
import jax.numpy as jnp
from jax import lax
from jax.sharding import PartitionSpec as P


def swapped(block, axis, apart):
    count = lax.axis_size(axis)
    route = []
    for low in range(count):
        high = low | 1 << apart
        if high != low and high < count:
            route += [(low, high), (high, low)]
    return lax.ppermute(block, axis, route)


def solve_factor(factor, values):
    middle = lax.linalg.triangular_solve(factor, values, left_side=True, lower=True)
    return lax.linalg.triangular_solve(factor, middle, left_side=True, lower=True, transpose_a=True)


def pair_sums(sums, bit_count):
    for step_bit in range(bit_count):
        partner = swapped((sums[0], sums[1]), "leaf", step_bit)
        sums = (sums[0] + partner[0], sums[1] + partner[1])
    return sums


def merge_level(height, level_basis, level_solved, carried):
    highest = lax.Precision.HIGHEST
    inner = (((1,), (1,)), ((), ()))
    capacity = lax.dot_general(level_basis, level_solved, inner, precision=highest)
    projected = lax.dot_general(level_basis, carried, inner, precision=highest)
    capacity, projected = pair_sums((capacity, projected), height + 1)
    capacity = capacity + jnp.eye(capacity.shape[0], dtype=jnp.float32)
    factor = jnp.linalg.cholesky(capacity)
    weights = solve_factor(factor, projected)
    update = lax.dot_general(weights, level_solved, (((0,), (0,)), ((), ())), precision=highest)
    return carried - update


def local(right_sides, leaf_inverse, bases, ordering):
    highest = lax.Precision.HIGHEST
    own_rows = right_sides.shape[0]
    piece_cols = leaf_inverse.shape[1]
    levels = bases.shape[0]
    basis_rank = bases.shape[1]
    groups = lax.axis_size("rhs")
    position = lax.axis_index("rhs")
    tree_order = jnp.take(right_sides, ordering[0], axis=1)
    tree_cols = lax.all_to_all(tree_order, "rhs", split_axis=1, concat_axis=0, tiled=True)
    basis_cols = lax.dynamic_slice_in_dim(bases, position * piece_cols, piece_cols, 2).astype(
        jnp.float32
    )
    column_share = basis_rank // groups
    split_basis = basis_cols.reshape(levels, groups, column_share, piece_cols)
    split_basis = split_basis.transpose(1, 0, 2, 3).reshape(
        groups, levels * column_share, piece_cols
    )
    stacked = jnp.concatenate([tree_cols.reshape(groups, own_rows, piece_cols), split_basis], 1)
    stacked = stacked.reshape(groups * (own_rows + levels * column_share), piece_cols)
    owned = lax.psum_scatter(
        lax.dot_general(stacked, leaf_inverse, (((1,), (1,)), ((), ())), precision=highest),
        "rhs",
        scatter_dimension=0,
        tiled=True,
    )
    solved = owned[:own_rows]
    pending = [
        owned[own_rows + offset * column_share : own_rows + (offset + 1) * column_share]
        for offset in range(levels)
    ]
    for height in range(levels):
        gathered = lax.all_gather(pending[height], "rhs", axis=0, tiled=True)
        carried = jnp.concatenate([solved] + pending[height + 1 :], 0)
        carried = merge_level(height, bases[height].astype(jnp.float32), gathered, carried)
        solved = carried[:own_rows]
        later = [
            carried[own_rows + offset * column_share : own_rows + (offset + 1) * column_share]
            for offset in range(levels - height - 1)
        ]
        pending = pending[: height + 1] + later
    result = jnp.zeros_like(solved).at[:, ordering[0]].set(solved)
    return result


def solution(mesh):
    placed = (P("rhs", "leaf"), P("leaf", "rhs"), P(None, None, "leaf"), P("leaf", None))
    return jax.shard_map(
        local, mesh=mesh, in_specs=placed, out_specs=P("rhs", "leaf"), check_vma=False
    )
```

profile of v0, /device:TPU:0, one launch (start us, length us, event | category | flops | bytes accessed | tf_op | source)
XLA Modules:
  0.0 195.7 jit_solution(8407929975835868010)
XLA Ops:
  7.9 1.3 reduce.7
  9.3 1.0 copy.19
  10.3 2.8 %gather_fusion = f32[1024,16]{1,0:T(8,128)S(1)} fusion(f32[16,1024]{0,1:T(8,128)S(1)} %copy.19, s32[1024]{0:T(1024)S(1)} %broadcast_clamp_fusion), kind=kCustom, calls=%fused_computation | custom fusion | bytes 135168 | tf_op jit(solution)/shard_map/jit(_take)/gather | solution.py:50
  13.9 4.2 %all-to-all-start = ((f32[16,4,256]{2,0,1:T(8,128)}), f32[16,4,256]{2,0,1:T(8,128)S(1)}, u32[]{:S(2)}, u32[]{:S(2)}) async-start(f32[16,4,256]{2,0,1:T(8,128)} %broadcast_select_fusion), calls=%async_computation | async-start | bytes 131072 | tf_op jit(solution)/shard_map/all_to_all | solution.py:51
  18.3 4.0 %all-to-all-done = f32[16,4,256]{2,0,1:T(8,128)S(1)} async-done(((f32[16,4,256]{2,0,1:T(8,128)}), f32[16,4,256]{2,0,1:T(8,128)S(1)}, u32[]{:S(2)}, u32[]{:S(2)}) %all-to-all-start) | async-done | bytes 65568 | tf_op jit(solution)/shard_map/all_to_all | solution.py:51
  22.3 2.9 %fusion.40 = f32[448,1024]{1,0:T(8,128)} fusion(f32[448,256]{1,0:T(8,128)S(1)} %bitcast.90, f32[1024,256]{1,0:T(8,128)S(1)} %copy-done), kind=kOutput, calls=%fused_computation.79 | convolution fusion | flops 1409286144 | bytes 3342336 | tf_op jit(solution)/shard_map/dot_general | solution.py:63
  25.3 30.6 %reduce-scatter.2.cloned.1.call-done = f32[112,1024]{1,0:T(8,128)} async-done(((f32[448,1024]{1,0:T(8,128)}), f32[112,1024]{1,0:T(8,128)}) %reduce-scatter.2.cloned.1.call-update) | async-done | bytes 458768 | tf_op jit(solution)/shard_map/reduce_scatter | solution.py:62
  56.9 6.6 %all_gather.9 = f32[128,1024]{1,0:T(8,128)S(1)} all-gather(f32[32,1024]{1,0:T(8,128)S(1)} %slice.78), channel_id=1, replica_groups=mesh['leaf'=8,'rhs'=4] {'rhs'}, dimensions={0}, use_global_device_ids=true | all-gather | bytes 655360 | tf_op jit(solution)/shard_map/all_gather | solution.py:74
  63.9 1.5 collective-permute-start
  68.4 11.7 %cholesky.59 = f32[128,128]{1,0:T(8,128)S(1)} custom-call(f32[128,128]{1,0:T(8,128)S(1)} %fusion.32), custom_call_target="Cholesky" | custom-call | tf_op jit(solution)/shard_map/jit(cholesky)/cholesky | solution.py:36
  81.5 9.8 %custom-call.17 = f32[1,128,128]{1,2,0:T(8,128)S(1)} custom-call(f32[1,128,128]{2,1,0:T(8,128)S(1)} %fusion.15), custom_call_target="InvertDiagBlocksLowerTriangular" | custom-call | tf_op jit(solution)/shard_map/triangular_solve | solution.py:19
  92.2 7.0 %all_gather.10 = f32[128,1024]{1,0:T(8,128)S(1)} all-gather(f32[32,1024]{1,0:T(8,128)S(1)} %get-tuple-element.7), channel_id=1, replica_groups=mesh['leaf'=8,'rhs'=4] {'rhs'}, dimensions={0}, use_global_device_ids=true | all-gather | bytes 655360 | tf_op jit(solution)/shard_map/all_gather | solution.py:74
  99.6 1.6 collective-permute-start.2
  101.1 2.9 %collective-permute-done.2 = f32[128,128]{0,1:T(8,128)S(1)} collective-permute-done((f32[128,128]{0,1:T(8,128)S(1)}, f32[128,128]{0,1:T(8,128)S(1)}, u32[]{:S(2)}, u32[]{:S(2)}) %collective-permute-start.2) | collective-permute-done | bytes 65568 | tf_op jit(solution)/shard_map/ppermute | solution.py:14
  104.0 1.6 collective-permute-start.3
  105.9 1.5 collective-permute-start.4
  107.5 2.4 %collective-permute-done.4 = f32[128,48]{0,1:T(8,128)S(1)} collective-permute-done((f32[128,48]{0,1:T(8,128)S(1)}, f32[128,48]{0,1:T(8,128)S(1)}, u32[]{:S(2)}, u32[]{:S(2)}) %collective-permute-start.4) | collective-permute-done | bytes 24608 | tf_op jit(solution)/shard_map/ppermute | solution.py:14
  110.5 11.7 %cholesky.70 = f32[128,128]{1,0:T(8,128)S(1)} custom-call(f32[128,128]{1,0:T(8,128)S(1)} %fusion.27), custom_call_target="Cholesky" | custom-call | tf_op jit(solution)/shard_map/jit(cholesky)/cholesky | solution.py:36
  123.6 9.8 %custom-call.18 = f32[1,128,128]{1,2,0:T(8,128)S(1)} custom-call(f32[1,128,128]{2,1,0:T(8,128)S(1)} %fusion.16), custom_call_target="InvertDiagBlocksLowerTriangular" | custom-call | tf_op jit(solution)/shard_map/triangular_solve | solution.py:19
  134.2 6.8 %all_gather.11 = f32[128,1024]{1,0:T(8,128)S(1)} all-gather(f32[32,1024]{1,0:T(8,128)S(1)} %slice.83), channel_id=1, replica_groups=mesh['leaf'=8,'rhs'=4] {'rhs'}, dimensions={0}, use_global_device_ids=true | all-gather | bytes 655360 | tf_op jit(solution)/shard_map/all_gather | solution.py:74
  141.4 1.5 collective-permute-start.6
  143.0 2.9 %collective-permute-done.6 = f32[128,128]{0,1:T(8,128)S(1)} collective-permute-done((f32[128,128]{0,1:T(8,128)S(1)}, f32[128,128]{0,1:T(8,128)S(1)}, u32[]{:S(2)}, u32[]{:S(2)}) %collective-permute-start.6) | collective-permute-done | bytes 65568 | tf_op jit(solution)/shard_map/ppermute | solution.py:14
  145.9 1.6 collective-permute-start.7
  147.4 2.8 %collective-permute-done.7 = f32[128,128]{0,1:T(8,128)S(1)} collective-permute-done((f32[128,128]{0,1:T(8,128)S(1)}, f32[128,128]{0,1:T(8,128)S(1)}, u32[]{:S(2)}, u32[]{:S(2)}) %collective-permute-start.7) | collective-permute-done | bytes 65568 | tf_op jit(solution)/shard_map/ppermute | solution.py:14
  150.2 2.5 %collective-permute-start.8 = (f32[128,128]{0,1:T(8,128)S(1)}, f32[128,128]{0,1:T(8,128)S(1)}, u32[]{:S(2)}, u32[]{:S(2)}) collective-permute-start(f32[128,128]{0,1:T(8,128)S(1)} %add.107), channel_id=1, source_target_pairs={{0,16},{16,0},{4,20},{20,4},{8,24},{24,8},{12,28},{28,12},{1,17},{... | collective-permute-start | bytes 196616 | tf_op jit(solution)/shard_map/ppermute | solution.py:14
  153.0 1.5 collective-permute-start.9
  154.5 2.2 %collective-permute-done.9 = f32[128,16]{0,1:T(8,128)S(1)} collective-permute-done((f32[128,16]{0,1:T(8,128)S(1)}, f32[128,16]{0,1:T(8,128)S(1)}, u32[]{:S(2)}, u32[]{:S(2)}) %collective-permute-start.9) | collective-permute-done | bytes 8224 | tf_op jit(solution)/shard_map/ppermute | solution.py:14
  156.7 1.5 collective-permute-start.10
  158.1 2.2 %collective-permute-done.10 = f32[128,16]{0,1:T(8,128)S(1)} collective-permute-done((f32[128,16]{0,1:T(8,128)S(1)}, f32[128,16]{0,1:T(8,128)S(1)}, u32[]{:S(2)}, u32[]{:S(2)}) %collective-permute-start.10) | collective-permute-done | bytes 8224 | tf_op jit(solution)/shard_map/ppermute | solution.py:14
  161.0 11.7 %cholesky.81 = f32[128,128]{1,0:T(8,128)S(1)} custom-call(f32[128,128]{1,0:T(8,128)S(1)} %fusion.22), custom_call_target="Cholesky" | custom-call | tf_op jit(solution)/shard_map/jit(cholesky)/cholesky | solution.py:36
  174.0 9.8 %custom-call.19 = f32[1,128,128]{1,2,0:T(8,128)S(1)} custom-call(f32[1,128,128]{2,1,0:T(8,128)S(1)} %fusion.17), custom_call_target="InvertDiagBlocksLowerTriangular" | custom-call | tf_op jit(solution)/shard_map/triangular_solve | solution.py:19
  184.8 3.2 %scatter_custom_fusion = f32[16,1024]{0,1:T(8,128)S(1)} fusion(s32[1024]{0:T(1024)S(1)} %bitcast.96, f32[1024,16]{1,0:T(8,128)S(1)} %copy.25, f32[]{:T(128)} %constant.71.clone.1), kind=kCustom, calls=%fused_computation.21 | custom fusion | bytes 65540 | tf_op jit(solution)/shard_map/scatter | solution.py:83
  (75 shorter events, 16.9 us)
Async XLA Ops:
  6.5 15.8 %copy-start = (f32[1024,256]{1,0:T(8,128)S(1)}, f32[1024,256]{1,0:T(8,128)}, u32[]{:S(2)}) copy-start(f32[1024,256]{1,0:T(8,128)} %param.6) | copy-start | bytes 3145732
  6.5 11.6 %copy-start.1 = (bf16[3,128,1024]{2,1,0:T(8,128)(2,1)S(1)}, bf16[3,128,1024]{2,1,0:T(8,128)(2,1)}, u32[]{:S(2)}) copy-start(bf16[3,128,1024]{2,1,0:T(8,128)(2,1)} %param.7) | copy-start | bytes 2359300
  13.9 8.4 %all-to-all-start = ((f32[16,4,256]{2,0,1:T(8,128)}), f32[16,4,256]{2,0,1:T(8,128)S(1)}, u32[]{:S(2)}, u32[]{:S(2)}) async-start(f32[16,4,256]{2,0,1:T(8,128)} %broadcast_select_fusion), calls=%async_computation | async-start | bytes 131072 | tf_op jit(solution)/shard_map/all_to_all | solution.py:51
  18.2 37.7 %reduce-scatter.2.cloned.1.call-start = ((), (), s32[]{:S(2)}) async-start(), calls=%async_computation.2 | async-start | bytes 2293760 | tf_op jit(solution)/shard_map/reduce_scatter | solution.py:62
  55.9 10.4 %copy-start.2 = (f32[112,1024]{1,0:T(8,128)S(1)}, f32[112,1024]{1,0:T(8,128)}, u32[]{:S(2)}) copy-start(f32[112,1024]{1,0:T(8,128)} %reduce-scatter.2.cloned.1.call-done) | copy-start | bytes 1376260
  63.9 4.4 %collective-permute-start = (f32[128,128]{0,1:T(8,128)S(1)}, f32[128,128]{0,1:T(8,128)S(1)}, u32[]{:S(2)}, u32[]{:S(2)}) collective-permute-start(f32[128,128]{0,1:T(8,128)S(1)} %convolution_bitcast_fusion.2), channel_id=1, source_target_pairs={{0,4},{4,0},{8,12},{12,8},{16,20},{20,16},{24,28},{28,24},{1,5},{5... | collective-permute-start | bytes 196616 | tf_op jit(solution)/shard_map/ppermute | solution.py:14
  66.7 24.6 %collective-permute-start.1 = (f32[128,80]{0,1:T(8,128)S(1)}, f32[128,80]{0,1:T(8,128)S(1)}, u32[]{:S(2)}, u32[]{:S(2)}) collective-permute-start(f32[128,80]{0,1:T(8,128)S(1)} %convolution_bitcast_fusion.3), channel_id=1, source_target_pairs={{0,4},{4,0},{8,12},{12,8},{16,20},{20,16},{24,28},{28,24},{1,5},{5... | collective-permute-start | bytes 122888 | tf_op jit(solution)/shard_map/ppermute | solution.py:14
  99.6 4.4 %collective-permute-start.2 = (f32[128,128]{0,1:T(8,128)S(1)}, f32[128,128]{0,1:T(8,128)S(1)}, u32[]{:S(2)}, u32[]{:S(2)}) collective-permute-start(f32[128,128]{0,1:T(8,128)S(1)} %convolution_bitcast_fusion.1), channel_id=1, source_target_pairs={{0,4},{4,0},{8,12},{12,8},{16,20},{20,16},{24,28},{28,24},{1,5},{5... | collective-permute-start | bytes 196616 | tf_op jit(solution)/shard_map/ppermute | solution.py:14
  104.0 6.4 %collective-permute-start.3 = (f32[128,128]{0,1:T(8,128)S(1)}, f32[128,128]{0,1:T(8,128)S(1)}, u32[]{:S(2)}, u32[]{:S(2)}) collective-permute-start(f32[128,128]{0,1:T(8,128)S(1)} %add.101), channel_id=1, source_target_pairs={{0,8},{8,0},{4,12},{12,4},{16,24},{24,16},{20,28},{28,20},{1,9},{9... | collective-permute-start | bytes 196616 | tf_op jit(solution)/shard_map/ppermute | solution.py:14
  105.9 3.9 %collective-permute-start.4 = (f32[128,48]{0,1:T(8,128)S(1)}, f32[128,48]{0,1:T(8,128)S(1)}, u32[]{:S(2)}, u32[]{:S(2)}) collective-permute-start(f32[128,48]{0,1:T(8,128)S(1)} %convolution_bitcast_fusion.4), channel_id=1, source_target_pairs={{0,4},{4,0},{8,12},{12,8},{16,20},{20,16},{24,28},{28,24},{1,5},{5... | collective-permute-start | bytes 73736 | tf_op jit(solution)/shard_map/ppermute | solution.py:14
  109.8 23.6 %collective-permute-start.5 = (f32[128,48]{0,1:T(8,128)S(1)}, f32[128,48]{0,1:T(8,128)S(1)}, u32[]{:S(2)}, u32[]{:S(2)}) collective-permute-start(f32[128,48]{0,1:T(8,128)S(1)} %add.104), channel_id=1, source_target_pairs={{0,8},{8,0},{4,12},{12,4},{16,24},{24,16},{20,28},{28,20},{1,9},{9... | collective-permute-start | bytes 73736 | tf_op jit(solution)/shard_map/ppermute | solution.py:14
  141.4 4.4 %collective-permute-start.6 = (f32[128,128]{0,1:T(8,128)S(1)}, f32[128,128]{0,1:T(8,128)S(1)}, u32[]{:S(2)}, u32[]{:S(2)}) collective-permute-start(f32[128,128]{0,1:T(8,128)S(1)} %convolution_bitcast_fusion), channel_id=1, source_target_pairs={{0,4},{4,0},{8,12},{12,8},{16,20},{20,16},{24,28},{28,24},{1,5},{5... | collective-permute-start | bytes 196616 | tf_op jit(solution)/shard_map/ppermute | solution.py:14
  145.9 4.3 %collective-permute-start.7 = (f32[128,128]{0,1:T(8,128)S(1)}, f32[128,128]{0,1:T(8,128)S(1)}, u32[]{:S(2)}, u32[]{:S(2)}) collective-permute-start(f32[128,128]{0,1:T(8,128)S(1)} %add.106), channel_id=1, source_target_pairs={{0,8},{8,0},{4,12},{12,4},{16,24},{24,16},{20,28},{28,20},{1,9},{9... | collective-permute-start | bytes 196616 | tf_op jit(solution)/shard_map/ppermute | solution.py:14
  150.2 10.6 %collective-permute-start.8 = (f32[128,128]{0,1:T(8,128)S(1)}, f32[128,128]{0,1:T(8,128)S(1)}, u32[]{:S(2)}, u32[]{:S(2)}) collective-permute-start(f32[128,128]{0,1:T(8,128)S(1)} %add.107), channel_id=1, source_target_pairs={{0,16},{16,0},{4,20},{20,4},{8,24},{24,8},{12,28},{28,12},{1,17},{... | collective-permute-start | bytes 196616 | tf_op jit(solution)/shard_map/ppermute | solution.py:14
  153.0 3.7 %collective-permute-start.9 = (f32[128,16]{0,1:T(8,128)S(1)}, f32[128,16]{0,1:T(8,128)S(1)}, u32[]{:S(2)}, u32[]{:S(2)}) collective-permute-start(f32[128,16]{0,1:T(8,128)S(1)} %convolution_bitcast_fusion.5), channel_id=1, source_target_pairs={{0,4},{4,0},{8,12},{12,8},{16,20},{20,16},{24,28},{28,24},{1,5},{5... | collective-permute-start | bytes 24584 | tf_op jit(solution)/shard_map/ppermute | solution.py:14
  156.7 3.7 %collective-permute-start.10 = (f32[128,16]{0,1:T(8,128)S(1)}, f32[128,16]{0,1:T(8,128)S(1)}, u32[]{:S(2)}, u32[]{:S(2)}) collective-permute-start(f32[128,16]{0,1:T(8,128)S(1)} %add.110), channel_id=1, source_target_pairs={{0,8},{8,0},{4,12},{12,4},{16,24},{24,16},{20,28},{28,20},{1,9},{9... | collective-permute-start | bytes 24584 | tf_op jit(solution)/shard_map/ppermute | solution.py:14
  160.3 23.5 %collective-permute-start.11 = (f32[128,16]{0,1:T(8,128)S(1)}, f32[128,16]{0,1:T(8,128)S(1)}, u32[]{:S(2)}, u32[]{:S(2)}) collective-permute-start(f32[128,16]{0,1:T(8,128)S(1)} %add.111), channel_id=1, source_target_pairs={{0,16},{16,0},{4,20},{20,4},{8,24},{24,8},{12,28},{28,12},{1,17},{... | collective-permute-start | bytes 24584 | tf_op jit(solution)/shard_map/ppermute | solution.py:14
Sparse Core Ops, SparseCore 0:
  25.4 30.4 reduce-scatter.1
where the time goes:
time: 196 us
  other arithmetic  71.6 us (37%)
  waiting for transfers between devices  50.9 us (26%)
  starting transfers between devices  20.6 us (11%)
  blocking collectives  20.4 us (10%)
  between operations  13.7 us (7%)
  local copies, waits for them, and re-layouts  11 us (6%)
  matrix products  7.58 us (4%)
    another operation x9, other arithmetic, merge_level(): factor = jnp.linalg.cholesky(capacity)  37.2 us
    another operation x6, other arithmetic, solve_factor(): lax.linalg.triangular_solve(factor, middle, left_side=True, lower=True, t...  31.4 us
    reduce_scatter x1, waiting for transfers between devices, local(): lax.psum_scatter(lax.dot_general(stacked, leaf_inverse, (((1,), (1,)), ((...  30.6 us
    all_gather x3, blocking collectives, local(): gathered = lax.all_gather(pending[height], 'rhs', axis=0, tiled=True)  20.4 us
    ppermute x12, starting transfers between devices, swapped(): return lax.ppermute(block, axis, route)  16.4 us
    ppermute x12, waiting for transfers between devices, swapped(): return lax.ppermute(block, axis, route)  16.2 us
    all_to_all x1, starting transfers between devices, local(): lax.all_to_all(tree_order, 'rhs', split_axis=1, concat_axis=0, tiled=True)  4.24 us
    scatter x2, local copies, waits for them, and re-layouts, local(): result = jnp.zeros_like(solved).at[:, ordering[0]].set(solved)  4.02 us
  transfers between devices with their start and end apart: 14, of which 9 were waited for; matrix products, arithmetic and copies ran while one was open for 36% of the time, Pallas kernels for 0%

commit v1 on v0

v1 whole, which is shorter than its diff:
```python
import functools

import jax
import jax.numpy as jnp
from jax import lax
from jax.experimental import pallas as pl
from jax.experimental.pallas import tpu as pltpu
from jax.sharding import PartitionSpec as P

F32 = jnp.float32
BF16 = jnp.bfloat16
NN = (((1,), (0,)), ((), ()))
NT = (((1,), (1,)), ((), ()))
STEP = 8


def split(value, pieces):
    parts = []
    for _ in range(pieces):
        head = value.astype(BF16)
        parts.append(head)
        value = value - head.astype(F32)
    return parts


def dot(left, right, dims):
    return lax.dot_general(left, right, dims, preferred_element_type=F32)


def fine(left, right, dims):
    return lax.dot_general(
        left, right, dims, precision=lax.Precision.HIGHEST, preferred_element_type=F32
    )


def inverse(matrix):
    size = matrix.shape[0]
    lane = lax.broadcasted_iota(jnp.int32, (1, size), 1)
    row_of = lax.broadcasted_iota(jnp.int32, (STEP, 1), 0)

    def block(_, a):
        for k in range(0, STEP, 2):
            first, second = a[k : k + 1], a[k + 1 : k + 2]
            a00 = jnp.broadcast_to(a[k : k + 1, k : k + 1], (1, size))
            a01 = jnp.broadcast_to(a[k : k + 1, k + 1 : k + 2], (1, size))
            a10 = jnp.broadcast_to(a[k + 1 : k + 2, k : k + 1], (1, size))
            a11 = jnp.broadcast_to(a[k + 1 : k + 2, k + 1 : k + 2], (1, size))
            scale = 1.0 / (a00 * a11 - a01 * a10)
            at0, at1 = lane == k, lane == k + 1
            first = jnp.where(at0, 1.0, jnp.where(at1, 0.0, first))
            second = jnp.where(at0, 0.0, jnp.where(at1, 1.0, second))
            new0 = (a11 * first - a01 * second) * scale
            new1 = (a00 * second - a10 * first) * scale
            col0, col1 = a[:, k : k + 1], a[:, k + 1 : k + 2]
            kept = jnp.where(at0 | at1, 0.0, a)
            a = kept - col0 * new0 - col1 * new1
            top = jnp.where(row_of == k, new0, jnp.where(row_of == k + 1, new1, a[:STEP]))
            a = jnp.concatenate([top, a[STEP:]], 0)
        a = jnp.concatenate([a[STEP:], a[:STEP]], 0)
        return pltpu.roll(a, size - STEP, 1)

    return lax.fori_loop(0, size // STEP, block, matrix)


def plan(leaves, groups, levels, rank, rows):
    units = [("c0", rank)]
    for j in range(levels):
        height = (levels - j) * rank - (rank if j == 0 else 0)
        if height:
            units.append((f"m{j}", height))
    units.append(("t", levels * rows))
    return units


def other(index, bit):
    return index + bit - 2 * bit * ((index // bit) % 2)


def kernel(cfg, rs_ref, g_ref, b_ref, ord_ref, out_ref, *scratch):
    leaves, groups, levels, rank, own_rows, points, piece = cfg
    rows = groups * own_rows
    units = plan(leaves, groups, levels, rank, rows)
    names = [name for name, _ in units]
    ref = dict(zip(scratch_names(cfg), scratch))
    leaf, position = lax.axis_index("leaf"), lax.axis_index("rhs")
    mesh_id = pl.DeviceIdType.MESH

    def at(leaf_index, rhs_index):
        return {"leaf": leaf_index, "rhs": rhs_index}

    rhs_peers = [lax.rem(position + k, groups) for k in range(1, groups)]
    mate = other(position, 1)
    half = lax.rem(position, 2)
    chips = [(leaf, lax.rem(position + k, groups)) for k in range(2, groups, 2)]
    chips += [(other(leaf, 1), lax.rem(position + k, groups)) for k in range(0, groups, 2)]
    greeted = [(leaf, p) for p in rhs_peers]
    greeted += chips[groups // 2 - 1 :]
    greeted += [(other(leaf, 1 << h), position) for h in range(1, levels)]

    barrier = pltpu.get_barrier_semaphore()
    for target in greeted:
        pl.semaphore_signal(barrier, inc=1, device_id=at(*target), device_id_type=mesh_id)

    def remote(src, dst, sems, slot, target):
        return pltpu.make_async_remote_copy(
            src_ref=src,
            dst_ref=dst,
            send_sem=ref[sems + "_s"].at[slot],
            recv_sem=ref[sems + "_r"].at[slot],
            device_id=at(*target),
            device_id_type=mesh_id,
        )

    g_parts = split(g_ref[...], 3)
    bases = b_ref[...].reshape(levels * rank, points)
    solved = dot(bases, g_parts[0], NN) + (dot(bases, g_parts[1], NN) + dot(bases, g_parts[2], NN))
    ref["y"][...] = solved
    own_cols = pl.ds(pl.multiple_of(position * piece, piece), piece)
    bases_own = b_ref[:, :, own_cols].reshape(levels * rank, piece)
    gram = sum(dot(part, bases_own, NT) for part in reversed(split(solved, 3)))
    for j in range(levels):
        column = gram[j * rank :, j * rank : (j + 1) * rank]
        if j == 0:
            ref["part_c0"][...] = column[:rank]
            column = column[rank:]
        if column.shape[0]:
            ref[f"part_m{j}"][...] = column

    pl.semaphore_wait(barrier, len(greeted))

    def halves(buffer, which):
        count = buffer.shape[0] // 2
        return buffer.at[pl.ds(pl.multiple_of(which * count, count), count)]

    def fold_start(name):
        slot = names.index(name)
        copy = remote(
            halves(ref["part_" + name], 1 - half), ref["fold_" + name], "fold", slot, (leaf, mate)
        )
        copy.start()
        return copy

    def spread_start(name, fold):
        fold.wait_recv()
        slot = names.index(name)
        ref["chip_" + name][...] = halves(ref["part_" + name], half)[...] + ref["fold_" + name][...]
        copies = []
        for k, target in enumerate(chips):
            copy = remote(
                ref["chip_" + name],
                ref["peer_" + name].at[k],
                "peer",
                slot * len(chips) + k,
                target,
            )
            copy.start()
            copies.append(copy)
        return copies

    def join_start(name, copies):
        for copy in copies:
            copy.wait_recv()
        total = ref["chip_" + name][...]
        for k in range(len(copies)):
            total = total + ref["peer_" + name][k]
        halves(ref["full_" + name], half)[...] = total
        slot = names.index(name)
        copy = remote(
            halves(ref["full_" + name], half),
            halves(ref["full_" + name], half),
            "join",
            slot,
            (leaf, mate),
        )
        copy.start()
        return copy

    folds = {name: fold_start(name) for name in names[:-1]}
    sent = []
    for k, peer in enumerate(rhs_peers):
        copy = remote(rs_ref, ref["rs"].at[position], "rs", k, (leaf, peer))
        copy.start()
        sent.append(copy)
    ref["rs"][position] = rs_ref[...]
    spreads = {"c0": spread_start("c0", folds["c0"])}

    tile = rank
    order = ord_ref[...]

    def one_hot(i, carry):
        start = pl.multiple_of(i * tile, tile)
        index = lax.broadcasted_iota(jnp.int32, (tile, points), 0) + start
        ref["perm"][pl.ds(start, tile), :] = jnp.where(index == order, 1.0, 0.0).astype(BF16)
        return carry

    lax.fori_loop(0, points // tile, one_hot, 0)
    for name in names[1:-1]:
        spreads[name] = spread_start(name, folds[name])

    for copy in sent:
        copy.wait_recv()
    gathered = ref["rs"][...].reshape(rows, points)
    tree = dot(jnp.concatenate(split(gathered, 3), 0), ref["perm"][...], NN).astype(BF16)
    by_0 = dot(tree, g_parts[0], NN)
    by_1 = dot(tree[: 2 * rows], g_parts[1], NN)
    by_2 = dot(tree[:rows], g_parts[2], NN)
    plain = by_0[:rows] + (
        (by_0[rows : 2 * rows] + by_1[:rows]) + (by_0[2 * rows :] + by_1[rows:] + by_2)
    )
    ref["x"][...] = plain
    term = sum(dot(part, bases_own, NT) for part in reversed(split(plain, 3)))
    for j in range(levels):
        ref["part_t"][j * rows : (j + 1) * rows] = term[:, j * rank : (j + 1) * rank]
    folds["t"] = fold_start("t")

    joins = {"c0": join_start("c0", spreads["c0"])}
    spreads["t"] = spread_start("t", folds["t"])
    eye = (
        lax.broadcasted_iota(jnp.int32, (rank, rank), 0)
        == lax.broadcasted_iota(jnp.int32, (rank, rank), 1)
    ).astype(F32)
    joins["c0"].wait_recv()

    level_copies = {}
    weights = []
    exchanged = []
    for h in range(levels):
        if h == 0:
            capacity = ref["full_c0"][...]
        else:
            level_copies[h, h, 0].wait_recv()
            capacity = ref[f"send{h}_{h}"][:rank] + ref[f"get{h}_{h}"][:rank]
        inverted = inverse(capacity + eye)
        if h == 0:
            for name in names[1:]:
                joins[name] = join_start(name, spreads[name])
            for name in names[1:]:
                joins[name].wait_recv()
            columns = []
            for j in range(levels):
                terms = [ref["full_t"][j * rows : (j + 1) * rows]]
                if f"m{j}" in names:
                    terms = [ref[f"full_m{j}"][...]] + terms
                columns.append(jnp.concatenate(terms, 0))
        else:
            columns = []
            for j in range(h, levels):
                start = rank if j == h else 0
                level_copies[h, j, 1].wait_recv()
                columns.append(ref[f"send{h}_{j}"][start:] + ref[f"get{h}_{j}"][start:])
        rest = columns[0]
        weight = fine(rest, inverted, NN)
        weights.append(weight)
        for j in range(h + 1, levels):
            offset = (j - h - 1) * rank
            update = fine(weight[offset:], rest[offset : offset + rank], NT)
            ref[f"send{h + 1}_{j}"][...] = columns[j - h] - update
            target = (other(leaf, 1 << (h + 1)), position)
            spans = [(1, 0, update.shape[0])]
            if j == h + 1:
                spans = [(0, 0, rank), (1, rank, update.shape[0] - rank)]
            for which, start, count in spans:
                slot = 2 * len(exchanged) + which
                copy = remote(
                    ref[f"send{h + 1}_{j}"].at[pl.ds(start, count)],
                    ref[f"get{h + 1}_{j}"].at[pl.ds(start, count)],
                    "level",
                    slot,
                    target,
                )
                copy.start()
                level_copies[h + 1, j, which] = copy
            exchanged.append((h, j))

    coefficients = [None] * levels
    for h in reversed(range(levels)):
        value = weights[h][(levels - 1 - h) * rank :]
        for j in range(h + 1, levels):
            offset = (j - h - 1) * rank
            value = value - fine(coefficients[j], weights[h][offset : offset + rank], NN)
        coefficients[h] = value
    answer = ref["x"][...] - fine(jnp.concatenate(coefficients, 1), ref["y"][...], NN)
    ref["answer"][...] = answer.reshape(groups, own_rows, piece)
    last = []
    for k, peer in enumerate(rhs_peers):
        copy = remote(ref["answer"].at[peer], ref["final"].at[position], "last", k, (leaf, peer))
        copy.start()
        last.append(copy)
    ref["final"][position] = ref["answer"][position]
    for copy in last:
        copy.wait_recv()
    tree_rows = jnp.concatenate([ref["final"][k] for k in range(groups)], 1)
    moved = dot(jnp.concatenate(split(tree_rows, 3), 0), ref["perm"][...], NT)
    out_ref[...] = moved[:own_rows] + (moved[own_rows : 2 * own_rows] + moved[2 * own_rows :])

    for copy in sent + last + list(folds.values()) + list(joins.values()):
        copy.wait_send()
    for copies in spreads.values():
        for copy in copies:
            copy.wait_send()
    for copy in level_copies.values():
        copy.wait_send()


def scratch_list(cfg):
    leaves, groups, levels, rank, own_rows, points, piece = cfg
    rows = groups * own_rows
    units = plan(leaves, groups, levels, rank, rows)
    chips = groups - 1
    items = [
        ("y", pltpu.VMEM((levels * rank, piece), F32)),
        ("x", pltpu.VMEM((rows, piece), F32)),
        ("rs", pltpu.VMEM((groups, own_rows, points), F32)),
        ("perm", pltpu.VMEM((points, points), BF16)),
        ("answer", pltpu.VMEM((groups, own_rows, piece), F32)),
        ("final", pltpu.VMEM((groups, own_rows, piece), F32)),
    ]
    for name, height in units:
        items += [
            ("part_" + name, pltpu.VMEM((height, rank), F32)),
            ("fold_" + name, pltpu.VMEM((height // 2, rank), F32)),
            ("chip_" + name, pltpu.VMEM((height // 2, rank), F32)),
            ("peer_" + name, pltpu.VMEM((chips, height // 2, rank), F32)),
            ("full_" + name, pltpu.VMEM((height, rank), F32)),
        ]
    pairs = 0
    for h in range(1, levels):
        for j in range(h, levels):
            pairs += 1
            height = (levels - j) * rank + rows
            items.append((f"send{h}_{j}", pltpu.VMEM((height, rank), F32)))
            items.append((f"get{h}_{j}", pltpu.VMEM((height, rank), F32)))
    counts = {
        "rs": groups - 1,
        "last": groups - 1,
        "fold": len(units),
        "join": len(units),
        "peer": len(units) * chips,
        "level": max(1, 2 * pairs),
    }
    for name, count in counts.items():
        items.append((name + "_s", pltpu.SemaphoreType.DMA((count,))))
        items.append((name + "_r", pltpu.SemaphoreType.DMA((count,))))
    return items


def scratch_names(cfg):
    return [name for name, _ in scratch_list(cfg)]


def local(right_sides, leaf_inverse, bases, ordering):
    own_rows, points = right_sides.shape
    levels, rank = bases.shape[:2]
    cfg = (
        lax.axis_size("leaf"),
        lax.axis_size("rhs"),
        levels,
        rank,
        own_rows,
        points,
        leaf_inverse.shape[1],
    )
    return pl.pallas_call(
        functools.partial(kernel, cfg),
        out_shape=jax.ShapeDtypeStruct((own_rows, points), F32),
        in_specs=[pl.BlockSpec(memory_space=pltpu.VMEM)] * 4,
        out_specs=pl.BlockSpec(memory_space=pltpu.VMEM),
        scratch_shapes=[item for _, item in scratch_list(cfg)],
        compiler_params=pltpu.CompilerParams(collective_id=0, has_side_effects=True),
        name="tree_solve",
    )(right_sides, leaf_inverse, bases, ordering)


def solution(mesh):
    placed = (P("rhs", "leaf"), P("leaf", "rhs"), P(None, None, "leaf"), P("leaf", None))
    return jax.shard_map(
        local, mesh=mesh, in_specs=placed, out_specs=P("rhs", "leaf"), check_vma=False
    )
```

time: 196 us -> 56.4 us (0.29)
  other arithmetic: 71.6 us -> 0 us
  Pallas kernels: 0 us -> 54.8 us
  waiting for transfers between devices: 50.9 us -> 0 us
  starting transfers between devices: 20.6 us -> 0 us
  blocking collectives: 20.4 us -> 0 us
  between operations: 13.7 us -> 0.01 us
  local copies, waits for them, and re-layouts: 11 us -> 1.47 us
  matrix products: 7.58 us -> 0 us
    another operation x15 -> x0, other arithmetic: 68.6 us -> none  [the longest x9 37.2 us: merge_level(): factor = jnp.linalg.cholesky(capacity)]
    pallas_call x0 -> x1, Pallas kernels: none -> 54.8 us  [local(): pl.pallas_call(functools.partial(kernel, cfg), out_shape=jax.ShapeDtypeSt...]
    reduce_scatter x1 -> x0, waiting for transfers between devices: 30.6 us -> none  [local(): lax.psum_scatter(lax.dot_general(stacked, leaf_inverse, (((1,), (1,)), ((...]
    all_gather x3 -> x0, blocking collectives: 20.4 us -> none  [local(): gathered = lax.all_gather(pending[height], 'rhs', axis=0, tiled=True)]
    ppermute x12 -> x0, starting transfers between devices: 16.4 us -> none  [swapped(): return lax.ppermute(block, axis, route)]
    ppermute x12 -> x0, waiting for transfers between devices: 16.2 us -> none  [swapped(): return lax.ppermute(block, axis, route)]
    dot_general x10 -> x0, matrix products: 6.4 us -> none  [the longest x1 2.92 us: local(): lax.dot_general(stacked, leaf_inverse, (((1,), (1,)), ((), ())), precisio...]
    all_to_all x1 -> x0, starting transfers between devices: 4.24 us -> none  [local(): lax.all_to_all(tree_order, 'rhs', split_axis=1, concat_axis=0, tiled=True)]
  transfers between devices with their start and end apart: 14 -> 0, of which waited for: 9 -> 0; matrix products, arithmetic and copies ran while one was open for 36% -> 0% of each run, Pallas kernels for 0% -> 0%
where the time goes in v1:
time: 56.4 us; the launch traced here: 56.2 us
  Pallas kernels  54.8 us (97%)
  local copies, waits for them, and re-layouts  1.47 us (3%)
    pallas_call x1, Pallas kernels, local(): pl.pallas_call(functools.partial(kernel, cfg), out_shape=jax.ShapeDtypeSt...  54.8 us
    unnamed x1, local copies, waits for them, and re-layouts  1.47 us

profile of v1, /device:TPU:0, one launch (start us, length us, event | category | flops | bytes accessed | tf_op | source)
XLA Modules:
  0.0 56.2 jit_solution(9313942434634224066)
XLA Ops:
  0.0 54.8 %tree_solve.1 = f32[16,1024]{1,0:T(8,128)} custom-call(f32[16,1024]{1,0:T(8,128)} %rs_ref.1, f32[1024,256]{1,0:T(8,128)} %g_ref.1, bf16[3,128,1024]{2,1,0:T(8,128)(2,1)} %b_ref.1, s32[1,1024]{1,0:T(1,128)} %ord_ref.1), custom_call_target="tpu_custom_call" | custom-call | tf_op jit(solution)/shard_map/tree_solve/pallas_call | solution.py:363
  54.8 1.5 %copy.6 = f32[16,1024]{1,0:T(8,128)} copy(f32[16,1024]{1,0:T(8,128)} %tree_solve.1) | data formatting | bytes 131072

commit v2 on v1

--- a/solution.py
+++ b/solution.py
@@ -63,13 +63,20 @@
 
 
 def plan(leaves, groups, levels, rank, rows):
-    units = [("c0", rank)]
+    early = [("c0", rank)]
+    late = []
     for j in range(levels):
-        height = (levels - j) * rank - (rank if j == 0 else 0)
+        height = (levels - j) * rank
+        if j == 1:
+            early.append(("c1", rank))
+        if j < 2:
+            height -= rank
         if height:
-            units.append((f"m{j}", height))
-    units.append(("t", levels * rows))
-    return units
+            (late if j else early).append((f"m{j}", height))
+    early.append(("t0", rows))
+    if levels > 1:
+        late.append(("t1", (levels - 1) * rows))
+    return early, late
 
 
 def other(index, bit):
@@ -79,8 +86,9 @@
 def kernel(cfg, rs_ref, g_ref, b_ref, ord_ref, out_ref, *scratch):
     leaves, groups, levels, rank, own_rows, points, piece = cfg
     rows = groups * own_rows
-    units = plan(leaves, groups, levels, rank, rows)
-    names = [name for name, _ in units]
+    early, late = plan(leaves, groups, levels, rank, rows)
+    early, late = [name for name, _ in early], [name for name, _ in late]
+    names = early + late
     ref = dict(zip(scratch_names(cfg), scratch))
     leaf, position = lax.axis_index("leaf"), lax.axis_index("rhs")
     mesh_id = pl.DeviceIdType.MESH
@@ -112,6 +120,8 @@
         )
 
     g_parts = split(g_ref[...], 3)
+    for k, part in enumerate(g_parts):
+        ref[f"g{k}"][...] = part
     bases = b_ref[...].reshape(levels * rank, points)
     solved = dot(bases, g_parts[0], NN) + (dot(bases, g_parts[1], NN) + dot(bases, g_parts[2], NN))
     ref["y"][...] = solved
@@ -120,8 +130,8 @@
     gram = sum(dot(part, bases_own, NT) for part in reversed(split(solved, 3)))
     for j in range(levels):
         column = gram[j * rank :, j * rank : (j + 1) * rank]
-        if j == 0:
-            ref["part_c0"][...] = column[:rank]
+        if j < 2:
+            ref[f"part_c{j}"][...] = column[:rank]
             column = column[rank:]
         if column.shape[0]:
             ref[f"part_m{j}"][...] = column
@@ -175,14 +185,8 @@
         copy.start()
         return copy
 
-    folds = {name: fold_start(name) for name in names[:-1]}
-    sent = []
-    for k, peer in enumerate(rhs_peers):
-        copy = remote(rs_ref, ref["rs"].at[position], "rs", k, (leaf, peer))
-        copy.start()
-        sent.append(copy)
-    ref["rs"][position] = rs_ref[...]
-    spreads = {"c0": spread_start("c0", folds["c0"])}
+    grams = [name for name in names if not name.startswith("t")]
+    folds = {name: fold_start(name) for name in grams}
 
     tile = rank
     order = ord_ref[...]
@@ -194,27 +198,56 @@
         return carry
 
     lax.fori_loop(0, points // tile, one_hot, 0)
-    for name in names[1:-1]:
+    spreads = {"c0": spread_start("c0", folds["c0"])}
+    moved = dot(jnp.concatenate(split(rs_ref[...], 3), 0), ref["perm"][...], NN)
+    ref["tree"][...] = (moved[:own_rows] + moved[own_rows : 2 * own_rows]) + moved[2 * own_rows :]
+    pieces = []
+    for k, peer in enumerate(rhs_peers):
+        copy = remote(
+            ref["tree"].at[:, pl.ds(pl.multiple_of(peer * piece, piece), piece)],
+            ref["cols"].at[position],
+            "cols",
+            k,
+            (leaf, peer),
+        )
+        copy.start()
+        pieces.append(copy)
+    ref["cols"][position] = ref["tree"][:, own_cols]
+    for name in early[1:]:
+        if name in grams:
+            spreads[name] = spread_start(name, folds[name])
+    for copy in pieces:
+        copy.wait_recv()
+    term = fine(ref["cols"][...].reshape(rows, piece), ref["y"][...], NT)
+    ref["part_t0"][...] = term[:, :rank]
+    folds["t0"] = fold_start("t0")
+    for j in range(1, levels):
+        ref["part_t1"][(j - 1) * rows : j * rows] = term[:, j * rank : (j + 1) * rank]
+    if levels > 1:
+        folds["t1"] = fold_start("t1")
+    spreads["t0"] = spread_start("t0", folds["t0"])
+    for name in late:
         spreads[name] = spread_start(name, folds[name])
-
-    for copy in sent:
-        copy.wait_recv()
-    gathered = ref["rs"][...].reshape(rows, points)
-    tree = dot(jnp.concatenate(split(gathered, 3), 0), ref["perm"][...], NN).astype(BF16)
-    by_0 = dot(tree, g_parts[0], NN)
-    by_1 = dot(tree[: 2 * rows], g_parts[1], NN)
-    by_2 = dot(tree[:rows], g_parts[2], NN)
-    plain = by_0[:rows] + (
-        (by_0[rows : 2 * rows] + by_1[:rows]) + (by_0[2 * rows :] + by_1[rows:] + by_2)
-    )
-    ref["x"][...] = plain
-    term = sum(dot(part, bases_own, NT) for part in reversed(split(plain, 3)))
-    for j in range(levels):
-        ref["part_t"][j * rows : (j + 1) * rows] = term[:, j * rank : (j + 1) * rank]
-    folds["t"] = fold_start("t")
+    sent = []
+    for k, peer in enumerate(rhs_peers):
+        copy = remote(ref["tree"], ref["rs"].at[position], "rs", k, (leaf, peer))
+        copy.start()
+        sent.append(copy)
+    ref["rs"][position] = ref["tree"][...]
+
+    def plain_term():
+        for copy in sent:
+            copy.wait_recv()
+        gathered = ref["rs"][...].reshape(rows, points)
+        stack = jnp.concatenate(split(gathered, 3), 0)
+        by_0 = dot(stack, ref["g0"][...], NN)
+        by_1 = dot(stack[: 2 * rows], ref["g1"][...], NN)
+        by_2 = dot(stack[:rows], ref["g2"][...], NN)
+        ref["x"][...] = by_0[:rows] + (
+            (by_0[rows : 2 * rows] + by_1[:rows]) + (by_0[2 * rows :] + by_1[rows:] + by_2)
+        )
 
     joins = {"c0": join_start("c0", spreads["c0"])}
-    spreads["t"] = spread_start("t", folds["t"])
     eye = (
         lax.broadcasted_iota(jnp.int32, (rank, rank), 0)
         == lax.broadcasted_iota(jnp.int32, (rank, rank), 1)
@@ -223,7 +256,24 @@
 
     level_copies = {}
     weights = []
-    exchanged = []
+    slots = iter(range(levels * levels * 2))
+
+    def level_start(h, j, which, start, value):
+        span = pl.ds(start, value.shape[0])
+        ref[f"send{h}_{j}"][span, :] = value
+        copy = remote(
+            ref[f"send{h}_{j}"].at[span],
+            ref[f"get{h}_{j}"].at[span],
+            "level",
+            next(slots),
+            (other(leaf, 1 << h), position),
+        )
+        copy.start()
+        level_copies[h, j, which] = copy
+
+    def level_value(h, j, start):
+        return ref[f"send{h}_{j}"][start:] + ref[f"get{h}_{j}"][start:]
+
     for h in range(levels):
         if h == 0:
             capacity = ref["full_c0"][...]
@@ -232,45 +282,49 @@
             capacity = ref[f"send{h}_{h}"][:rank] + ref[f"get{h}_{h}"][:rank]
         inverted = inverse(capacity + eye)
         if h == 0:
-            for name in names[1:]:
+            for name in early[1:]:
                 joins[name] = join_start(name, spreads[name])
-            for name in names[1:]:
+            for name in early[1:]:
                 joins[name].wait_recv()
-            columns = []
-            for j in range(levels):
-                terms = [ref["full_t"][j * rows : (j + 1) * rows]]
-                if f"m{j}" in names:
-                    terms = [ref[f"full_m{j}"][...]] + terms
-                columns.append(jnp.concatenate(terms, 0))
+            rest = ref["full_t0"][...]
+            if levels > 1:
+                rest = jnp.concatenate([ref["full_m0"][...], rest], 0)
+                head = ref["full_c1"][...]
         else:
-            columns = []
-            for j in range(h, levels):
-                start = rank if j == h else 0
-                level_copies[h, j, 1].wait_recv()
-                columns.append(ref[f"send{h}_{j}"][start:] + ref[f"get{h}_{j}"][start:])
-        rest = columns[0]
-        weight = fine(rest, inverted, NN)
+            level_copies[h, h, 1].wait_recv()
+            rest = level_value(h, h, rank)
+            if h + 1 < levels:
+                level_copies[h, h + 1, 1].wait_recv()
+                following = level_value(h, h + 1, 0)
+                head, tail = following[:rank], following[rank:]
+        if h + 1 < levels:
+            first = fine(rest[:rank], inverted, NN)
+            level_start(h + 1, h + 1, 0, 0, head - fine(first, rest[:rank], NT))
+            weight = jnp.concatenate([first, fine(rest[rank:], inverted, NN)], 0)
+        else:
+            weight = fine(rest, inverted, NN)
         weights.append(weight)
+        if h == 0:
+            for name in late:
+                joins[name] = join_start(name, spreads[name])
+            for name in late:
+                joins[name].wait_recv()
         for j in range(h + 1, levels):
             offset = (j - h - 1) * rank
-            update = fine(weight[offset:], rest[offset : offset + rank], NT)
-            ref[f"send{h + 1}_{j}"][...] = columns[j - h] - update
-            target = (other(leaf, 1 << (h + 1)), position)
-            spans = [(1, 0, update.shape[0])]
-            if j == h + 1:
-                spans = [(0, 0, rank), (1, rank, update.shape[0] - rank)]
-            for which, start, count in spans:
-                slot = 2 * len(exchanged) + which
-                copy = remote(
-                    ref[f"send{h + 1}_{j}"].at[pl.ds(start, count)],
-                    ref[f"get{h + 1}_{j}"].at[pl.ds(start, count)],
-                    "level",
-                    slot,
-                    target,
-                )
-                copy.start()
-                level_copies[h + 1, j, which] = copy
-            exchanged.append((h, j))
+            start = rank if j == h + 1 else 0
+            if h == 0:
+                column = ref["full_t1"][(j - 1) * rows : j * rows]
+                if f"m{j}" in names:
+                    column = jnp.concatenate([ref[f"full_m{j}"][...], column], 0)
+            elif j == h + 1:
+                column = tail
+            else:
+                level_copies[h, j, 1].wait_recv()
+                column = level_value(h, j, 0)
+            update = fine(weight[offset + start :], rest[offset : offset + rank], NT)
+            level_start(h + 1, j, 1, start, column - update)
+        if h == max(levels - 2, 0):
+            plain_term()
 
     coefficients = [None] * levels
     for h in reversed(range(levels)):
@@ -293,7 +347,7 @@
     moved = dot(jnp.concatenate(split(tree_rows, 3), 0), ref["perm"][...], NT)
     out_ref[...] = moved[:own_rows] + (moved[own_rows : 2 * own_rows] + moved[2 * own_rows :])
 
-    for copy in sent + last + list(folds.values()) + list(joins.values()):
+    for copy in pieces + sent + last + list(folds.values()) + list(joins.values()):
         copy.wait_send()
     for copies in spreads.values():
         for copy in copies:
@@ -305,12 +359,18 @@
 def scratch_list(cfg):
     leaves, groups, levels, rank, own_rows, points, piece = cfg
     rows = groups * own_rows
-    units = plan(leaves, groups, levels, rank, rows)
+    early, late = plan(leaves, groups, levels, rank, rows)
+    units = early + late
     chips = groups - 1
     items = [
         ("y", pltpu.VMEM((levels * rank, piece), F32)),
         ("x", pltpu.VMEM((rows, piece), F32)),
         ("rs", pltpu.VMEM((groups, own_rows, points), F32)),
+        ("tree", pltpu.VMEM((own_rows, points), F32)),
+        ("cols", pltpu.VMEM((groups, own_rows, piece), F32)),
+        ("g0", pltpu.VMEM((points, piece), BF16)),
+        ("g1", pltpu.VMEM((points, piece), BF16)),
+        ("g2", pltpu.VMEM((points, piece), BF16)),
         ("perm", pltpu.VMEM((points, points), BF16)),
         ("answer", pltpu.VMEM((groups, own_rows, piece), F32)),
         ("final", pltpu.VMEM((groups, own_rows, piece), F32)),
@@ -332,6 +392,7 @@
             items.append((f"get{h}_{j}", pltpu.VMEM((height, rank), F32)))
     counts = {
         "rs": groups - 1,
+        "cols": groups - 1,
         "last": groups - 1,
         "fold": len(units),
         "join": len(units),

time: 56.4 us -> 55.6 us (0.986)
  Pallas kernels: 54.8 us -> 53.9 us
    pallas_call x1, Pallas kernels: 54.8 us -> 53.9 us  [local(): pl.pallas_call(functools.partial(kernel, cfg), out_shape=jax.ShapeDtypeSt...]
where the time goes in v2:
time: 55.6 us; the launch traced here: 55.4 us
  Pallas kernels  53.9 us (97%)
  local copies, waits for them, and re-layouts  1.47 us (3%)
    pallas_call x1, Pallas kernels, local(): pl.pallas_call(functools.partial(kernel, cfg), out_shape=jax.ShapeDtypeSt...  53.9 us
    unnamed x1, local copies, waits for them, and re-layouts  1.47 us

profile of v2, /device:TPU:0, one launch (start us, length us, event | category | flops | bytes accessed | tf_op | source)
XLA Modules:
  0.0 55.4 jit_solution(9281553929510012809)
XLA Ops:
  0.0 53.9 %tree_solve.1 = f32[16,1024]{1,0:T(8,128)} custom-call(f32[16,1024]{1,0:T(8,128)} %rs_ref.1, f32[1024,256]{1,0:T(8,128)} %g_ref.1, bf16[3,128,1024]{2,1,0:T(8,128)(2,1)} %b_ref.1, s32[1,1024]{1,0:T(1,128)} %ord_ref.1), custom_call_target="tpu_custom_call" | custom-call | tf_op jit(solution)/shard_map/tree_solve/pallas_call | solution.py:424
  53.9 1.5 %copy.6 = f32[16,1024]{1,0:T(8,128)} copy(f32[16,1024]{1,0:T(8,128)} %tree_solve.1) | data formatting | bytes 131072

commit v3 on v2

--- a/solution.py
+++ b/solution.py
@@ -11,7 +11,8 @@
 BF16 = jnp.bfloat16
 NN = (((1,), (0,)), ((), ()))
 NT = (((1,), (1,)), ((), ()))
-STEP = 8
+STEP = 32
+TILE = 8
 
 
 def split(value, pieces):
@@ -36,7 +37,7 @@
 def inverse(matrix):
     size = matrix.shape[0]
     lane = lax.broadcasted_iota(jnp.int32, (1, size), 1)
-    row_of = lax.broadcasted_iota(jnp.int32, (STEP, 1), 0)
+    row_of = lax.broadcasted_iota(jnp.int32, (TILE, 1), 0)
 
     def block(_, a):
         for k in range(0, STEP, 2):
@@ -54,8 +55,12 @@
             col0, col1 = a[:, k : k + 1], a[:, k + 1 : k + 2]
             kept = jnp.where(at0 | at1, 0.0, a)
             a = kept - col0 * new0 - col1 * new1
-            top = jnp.where(row_of == k, new0, jnp.where(row_of == k + 1, new1, a[:STEP]))
-            a = jnp.concatenate([top, a[STEP:]], 0)
+            base = k // TILE * TILE
+            rows = a[base : base + TILE]
+            rows = jnp.where(row_of == k - base, new0, rows)
+            rows = jnp.where(row_of == k + 1 - base, new1, rows)
+            before = [a[:base]] if base else []
+            a = jnp.concatenate(before + [rows, a[base + TILE :]], 0)
         a = jnp.concatenate([a[STEP:], a[:STEP]], 0)
         return pltpu.roll(a, size - STEP, 1)
 

time: 55.6 us -> 52 us (0.935)
  Pallas kernels: 53.9 us -> 50.4 us
    pallas_call x1, Pallas kernels: 53.9 us -> 50.4 us  [local(): pl.pallas_call(functools.partial(kernel, cfg), out_shape=jax.ShapeDtypeSt...]
where the time goes in v3:
time: 52 us; the launch traced here: 51.9 us
  Pallas kernels  50.4 us (97%)
  local copies, waits for them, and re-layouts  1.47 us (3%)
    pallas_call x1, Pallas kernels, local(): pl.pallas_call(functools.partial(kernel, cfg), out_shape=jax.ShapeDtypeSt...  50.4 us
    unnamed x1, local copies, waits for them, and re-layouts  1.47 us

profile of v3, /device:TPU:0, one launch (start us, length us, event | category | flops | bytes accessed | tf_op | source)
XLA Modules:
  0.0 51.9 jit_solution(7214029706156762496)
XLA Ops:
  0.0 50.4 %tree_solve.1 = f32[16,1024]{1,0:T(8,128)} custom-call(f32[16,1024]{1,0:T(8,128)} %rs_ref.1, f32[1024,256]{1,0:T(8,128)} %g_ref.1, bf16[3,128,1024]{2,1,0:T(8,128)(2,1)} %b_ref.1, s32[1,1024]{1,0:T(1,128)} %ord_ref.1), custom_call_target="tpu_custom_call" | custom-call | tf_op jit(solution)/shard_map/tree_solve/pallas_call | solution.py:429
  50.4 1.5 %copy.6 = f32[16,1024]{1,0:T(8,128)} copy(f32[16,1024]{1,0:T(8,128)} %tree_solve.1) | data formatting | bytes 131072
